TPU v7x, 32 devices: a whole 2x2x4 slice. The times are simulated.
32 devices in a mesh: fact: 8 (over z, x), dim: 4 (over y, core).
Axes of the slice: x: 2, y: 2, z: 4, core: 2. Of those that a mesh axis runs over, the one named last changes fastest.
Arguments:
- fact_keys: int32 [1048576], P(('fact', 'dim')), may hold values from 0 to 65535, as said below
- revenue: bfloat16 [1048576], P(('fact', 'dim')), may hold values from 0.099609375 to 1
- filter_bits: int32 [256, 256], replicated, may hold values from 0 to 1
- categories: int32 [65536], P(('fact', 'dim')), may hold values from 0 to 511
- attributes: bfloat16 [65536, 128], P(('fact', 'dim')), may hold values from -0.125 to 0.125
Outputs:
- category_totals: float32 [512, 128], P(('fact', 'dim'))
Inputs may be any that keep to these rules, and one draw needn't show every extreme that they name: `fact_keys`: keys of owner o are o * 2048 to (o + 1) * 2048 - 1. Among the 32768 rows of one device at most 2048 have keys of any one owner; in every draw one owner gets exactly 2048 matching rows from every device, and every device has exactly 2048 matching rows for some owner.
All inputs are finite; a program needn't handle non-finite values.
Results may differ from a plain program's by a relative error of at most 0.0003.
Values may be sent and summed in bfloat16 or wider, within the bound.
No kernel may reach another device: no remote copies, remote signals or barrier semaphores. Data moves between devices by JAX's collectives and lax.ppermute only.
A program may use at most 64 MiB of HBM per device.

v0:
```python
import math

import jax
import jax.numpy as jnp
from jax import lax
from jax.sharding import PartitionSpec as P

CATS = 512


def category_sums(own_sums, categories, attributes):
    weighted = own_sums[:, None] * attributes.astype(jnp.float32)
    cat_hot = (categories[:, None] == jnp.arange(CATS, dtype=jnp.int32)[None, :]).astype(
        jnp.float32
    )
    return lax.dot_general(
        cat_hot,
        weighted,
        (((0,), (0,)), ((), ())),
        precision=lax.Precision.HIGHEST,
        preferred_element_type=jnp.float32,
    )


def per_device(fact_keys, revenue, filter_bits, categories, attributes):
    rows = fact_keys.shape[0]
    key_hi, key_lo = filter_bits.shape
    filt = filter_bits.astype(jnp.bfloat16)
    block = math.gcd(rows, 2048)
    keys_blocks = fact_keys.reshape(rows // block, block)
    rev_blocks = revenue.reshape(rows // block, block)
    high_ids = jnp.arange(key_hi, dtype=jnp.int32)
    low_ids = jnp.arange(key_lo, dtype=jnp.int32)
    zero_half = jnp.zeros((), jnp.bfloat16)

    def probe_block(item):
        keys, rev = item
        high = (keys[:, None] // key_lo == high_ids[None, :]).astype(jnp.bfloat16)
        low = keys[:, None] % key_lo == low_ids[None, :]
        passing = jnp.dot(high, filt, preferred_element_type=jnp.float32)
        match = jnp.sum(jnp.where(low, passing, 0.0), axis=1)
        return (high, low, match)

    def add_sums(carry, item):
        high, low, match = probe_block(item)
        scaled = item[1] * match.astype(jnp.bfloat16)
        weighted_low = jnp.where(low, scaled[:, None], zero_half)
        term = lax.dot_general(
            high, weighted_low, (((0,), (0,)), ((), ())), preferred_element_type=jnp.float32
        )
        return (carry + term, None)

    totals, _ = lax.scan(
        add_sums, jnp.zeros((key_hi, key_lo), jnp.float32), (keys_blocks, rev_blocks)
    )
    own_sums = lax.psum_scatter(
        totals.reshape(-1), ("fact", "dim"), scatter_dimension=0, tiled=True
    )
    partial_totals = category_sums(own_sums, categories, attributes)
    return lax.psum_scatter(partial_totals, ("fact", "dim"), scatter_dimension=0, tiled=True)


def solution(mesh):
    in_specs = (
        P(("fact", "dim")),
        P(("fact", "dim")),
        P(),
        P(("fact", "dim")),
        P(("fact", "dim"), None),
    )
    out_specs = P(("fact", "dim"), None)
    return jax.shard_map(
        per_device, mesh=mesh, in_specs=in_specs, out_specs=out_specs, check_vma=False
    )
```

profile of v0, /device:TPU:0, one launch (start us, length us, event | category | flops | bytes accessed | tf_op | source)
XLA Modules:
  0.0 311.7 jit_solution(16808163438264407972)
XLA Ops:
  6.5 0.0 copy-start
  6.5 0.0 all-reduce.3.cloned.1.call-start
  6.5 1.0 convert_element_type.20
  7.5 0.9 reshape.119
  8.5 0.0 copy-done
  8.5 25.7 %while.15 = (s32[]{:T(128)}, f32[256,256]{1,0:T(8,128)S(1)}, s32[16,2048]{1,0:T(8,128)S(1)}, bf16[16,2048]{1,0:T(8,128)(2,1)S(1)}, bf16[256,256]{1,0:T(8,128)(2,1)S(1)}, /*index=5*/s32[]{:T(128)}, s32[]{:T(128)}) while((s32[]{:T(128)}, f32[256,256]{1,0:T(8,128)S(1)}, s32[16,2048]{1,0:T(8,128)S(1)}, ...), condition=%wide.region_2.3_spmd.clone.clone, body=%wide.region_0.2_spmd.clone.clone.sunk | while | flops 540710912 | bytes 757855 | solution.py:53
  8.6 0.7 fusion.27
  9.4 0.7 fusion.28
  10.2 0.7 fusion.27
  11.0 0.7 fusion.28
  11.8 0.7 fusion.27
  12.6 0.7 fusion.28
  13.4 0.7 fusion.27
  14.2 0.7 fusion.28
  15.0 0.7 fusion.27
  15.8 0.7 fusion.28
  16.6 0.7 fusion.27
  17.4 0.7 fusion.28
  18.2 0.7 fusion.27
  19.0 0.7 fusion.28
  19.8 0.7 fusion.27
  20.6 0.7 fusion.28
  21.4 0.7 fusion.27
  22.2 0.7 fusion.28
  23.0 0.7 fusion.27
  23.8 0.7 fusion.28
  24.6 0.7 fusion.27
  25.4 0.7 fusion.28
  26.2 0.7 fusion.27
  27.0 0.7 fusion.28
  27.8 0.7 fusion.27
  28.6 0.7 fusion.28
  29.4 0.7 fusion.27
  30.2 0.7 fusion.28
  31.0 0.7 fusion.27
  31.8 0.7 fusion.28
  32.6 0.7 fusion.27
  33.4 0.7 fusion.28
  34.2 0.0 copy-start.1
  34.2 0.0 copy-start.2
  34.2 0.8 copy.8
  35.1 0.0 all-reduce.3.cloned.1.call-update
  35.1 0.0 reduce-scatter.2.cloned.1.call-start
  35.1 129.4 %all-reduce.3.cloned.1.call-done = f32[65536]{0:T(1024)} async-done(((f32[65536]{0:T(1024)}), f32[65536]{0:T(1024)}) %all-reduce.3.cloned.1.call-update) | async-done | bytes 262160
  164.6 0.7 dynamic-slice
  165.3 0.0 copy-done.1
  165.3 0.0 copy-done.2
  165.3 4.7 %fusion.15 = f32[512,128]{1,0:T(8,128)} fusion(s32[2048]{0:T(1024)S(1)} %copy-done.2, bf16[2048,128]{1,0:T(8,128)(2,1)S(1)} %copy-done.1, f32[2048]{0:T(1024)S(1)} %dynamic-slice), kind=kOutput, calls=%fused_computation.26 | convolution fusion | flops 1612185600 | bytes 802816 | tf_op jit(solution)/shard_map/dot_general | solution.py:16
  170.0 0.0 reduce-scatter.2.cloned.1.call-update
  170.0 134.8 %reduce-scatter.2.cloned.1.call-done = f32[16,128]{1,0:T(8,128)} async-done(((f32[512,128]{1,0:T(8,128)}), f32[16,128]{1,0:T(8,128)}) %reduce-scatter.2.cloned.1.call-update) | async-done | bytes 8208 | tf_op jit(solution)/shard_map/reduce_scatter | solution.py:60
  (66 shorter events, 1.3 us)
Async XLA Ops:
  6.5 1.9 copy-start
  6.5 158.0 %all-reduce.3.cloned.1.call-start = ((), (), s32[]{:S(2)}) async-start(), calls=%async_computation.2 | async-start | bytes 524288
  34.2 131.1 %copy-start.1 = (bf16[2048,128]{1,0:T(8,128)(2,1)S(1)}, bf16[2048,128]{1,0:T(8,128)(2,1)}, u32[]{:S(2)}) copy-start(bf16[2048,128]{1,0:T(8,128)(2,1)} %param.11) | copy-start | bytes 1572868
  34.2 131.1 %copy-start.2 = (s32[2048]{0:T(1024)S(1)}, s32[2048]{0:T(1024)}, u32[]{:S(2)}) copy-start(s32[2048]{0:T(1024)} %param.10) | copy-start | bytes 24580
  35.1 269.7 %reduce-scatter.2.cloned.1.call-start = ((), (), s32[]{:S(2)}) async-start(), calls=%async_computation.1 | async-start | bytes 270336 | tf_op jit(solution)/shard_map/reduce_scatter | solution.py:60
Sparse Core Ops, SparseCore 0:
  35.2 129.3 all-reduce.2
  170.1 134.6 reduce-scatter.1
where the time goes:
time: 312 us
  waiting for transfers between devices  264 us (85%)
  matrix products  28.3 us (9%)
  between operations  13.5 us (4%)
  local copies, waits for them, and re-layouts  3.44 us (1%)
    reduce_scatter x1, waiting for transfers between devices, per_device(): lax.psum_scatter(partial_totals, ('fact', 'dim'), scatter_dimension=0, ti...  135 us
    unnamed x3, waiting for transfers between devices  129 us
    dot_general x16, matrix products, add_sums(): lax.dot_general(high, weighted_low, (((0,), (0,)), ((), ())), preferred_e...  12 us
    dot_general x16, matrix products, probe_block(): passing = jnp.dot(high, filt, preferred_element_type=jnp.float32)  11.6 us
  transfers between devices with their start and end apart: 2, of which 2 were waited for; matrix products, arithmetic and copies ran while one was open for 0% of the time, Pallas kernels for 0%

commit v1 on v0

v1 whole, which is shorter than its diff:
```python
import jax
import jax.numpy as jnp
from jax import lax
from jax.experimental import pallas as pl
from jax.experimental.pallas import tpu as pltpu
from jax.sharding import PartitionSpec as P

CATS = 512
AXES = ("fact", "dim")
LANES = 128
SUB = 16
CHUNK = 16


def hot(values, size):
    iota = lax.broadcasted_iota(jnp.int32, (size // SUB, SUB, LANES), 0) * SUB
    iota = iota + lax.broadcasted_iota(jnp.int32, (size // SUB, SUB, LANES), 1)
    iota = iota.astype(jnp.float32).astype(jnp.bfloat16)
    row = jnp.broadcast_to(values, (SUB, LANES)).astype(jnp.float32).astype(jnp.bfloat16)
    return iota == row[None]


def key_kernel(keys_ref, rev_ref, out_ref):
    groups = keys_ref.shape[0]
    key_hi, key_lo = out_ref.shape
    out_ref[...] = jnp.zeros_like(out_ref)
    one = jnp.ones((), jnp.bfloat16)
    zero = jnp.zeros((), jnp.bfloat16)

    def body(g, carry):
        base = pl.multiple_of(g * CHUNK, CHUNK)
        keys = keys_ref[pl.ds(base, CHUNK), :]
        rev = rev_ref[pl.ds(base, CHUNK), :].astype(jnp.float32)
        high = keys // key_lo
        low = keys % key_lo
        lhs, rhs = [], []
        for j in range(CHUNK):
            lhs.append(
                jnp.where(hot(high[j : j + 1], key_hi), one, zero).reshape(key_hi, LANES)
            )
            row = jnp.broadcast_to(rev[j : j + 1], (SUB, LANES)).astype(jnp.bfloat16)
            rhs.append(
                jnp.where(hot(low[j : j + 1], key_lo), row[None], zero).reshape(key_lo, LANES)
            )
        out_ref[...] += lax.dot_general(
            jnp.concatenate(lhs, axis=1),
            jnp.concatenate(rhs, axis=1),
            (((1,), (1,)), ((), ())),
            preferred_element_type=jnp.float32,
        )
        return carry

    lax.fori_loop(0, groups // CHUNK, body, 0)


def key_sums(fact_keys, revenue, key_hi, key_lo):
    vmem = pl.BlockSpec(memory_space=pltpu.VMEM)
    return pl.pallas_call(
        key_kernel,
        in_specs=[vmem, vmem],
        out_specs=vmem,
        out_shape=jax.ShapeDtypeStruct((key_hi, key_lo), jnp.float32),
        name="key_sums",
    )(fact_keys.reshape(-1, LANES), revenue.reshape(-1, LANES))


def category_kernel(terms_ref, filt_ref, cats_ref, attrs_ref, out_ref):
    half = out_ref.shape[0] // 2
    cats = cats_ref[...]
    sums = jnp.where(filt_ref[...] == 1, jnp.sum(terms_ref[...], axis=0), 0.0)
    coarse = sums.astype(jnp.bfloat16).astype(jnp.float32)
    fine = sums - coarse
    zero = jnp.zeros((), jnp.bfloat16)
    parts = sums.shape[1] // LANES
    for part in range(2):
        lhs, rhs = [], []
        for j in range(cats.shape[0]):
            r, c = j // parts, (j % parts) * LANES
            mask = hot(cats[j : j + 1] - part * half, half)
            attrs = attrs_ref[j * LANES : (j + 1) * LANES, :]
            for piece in (coarse, fine):
                row = jnp.broadcast_to(piece[r : r + 1, c : c + LANES], (SUB, LANES))
                row = row.astype(jnp.bfloat16)[None]
                lhs.append(jnp.where(mask, row, zero).reshape(half, LANES))
                rhs.append(attrs)
        out_ref[part * half : (part + 1) * half, :] = jnp.dot(
            jnp.concatenate(lhs, axis=1),
            jnp.concatenate(rhs, axis=0),
            preferred_element_type=jnp.float32,
        )


def category_sums(terms, filt, categories, attributes):
    vmem = pl.BlockSpec(memory_space=pltpu.VMEM)
    return pl.pallas_call(
        category_kernel,
        in_specs=[vmem, vmem, vmem, vmem],
        out_specs=vmem,
        out_shape=jax.ShapeDtypeStruct((CATS, attributes.shape[1]), jnp.float32),
        name="category_sums",
    )(terms, filt, categories.reshape(-1, LANES), attributes)


def solution(mesh):
    devices = mesh.shape["fact"] * mesh.shape["dim"]

    def spread(partial):
        blocks = partial.reshape(devices, -1, partial.shape[1])
        return lax.all_to_all(blocks, AXES, 0, 0, tiled=True)

    def per_device(fact_keys, revenue, filter_bits, categories, attributes):
        key_hi, key_lo = filter_bits.shape
        terms = spread(key_sums(fact_keys, revenue, key_hi, key_lo))
        rows = terms.shape[1]
        filt = lax.dynamic_slice_in_dim(filter_bits, lax.axis_index(AXES) * rows, rows, 0)
        partial = category_sums(terms, filt, categories, attributes)
        return jnp.sum(spread(partial), axis=0)

    in_specs = (P(AXES), P(AXES), P(), P(AXES), P(AXES, None))
    return jax.shard_map(
        per_device, mesh=mesh, in_specs=in_specs, out_specs=P(AXES, None), check_vma=False
    )
```

time: 312 us -> 45.2 us (0.14)
  waiting for transfers between devices: 264 us -> 9.95 us
  matrix products: 28.3 us -> 0 us
  between operations: 13.5 us -> 0.03 us
  blocking collectives: 0 us -> 13.2 us
  Pallas kernels: 0 us -> 12.6 us
  starting transfers between devices: 0.04 us -> 7.33 us
    reduce_scatter x1 -> x0, waiting for transfers between devices: 135 us -> none  [per_device(): lax.psum_scatter(partial_totals, ('fact', 'dim'), scatter_dimension=0, ti...]
    unnamed x3 -> x0, waiting for transfers between devices: 129 us -> none
    dot_general x33 -> x0, matrix products: 28.3 us -> none  [the longest x16 12 us: add_sums(): lax.dot_general(high, weighted_low, (((0,), (0,)), ((), ())), preferred_e...]
    all_to_all x0 -> x1, blocking collectives: none -> 13.2 us  [spread(): return lax.all_to_all(blocks, AXES, 0, 0, tiled=True)]
    pallas_call x0 -> x2, Pallas kernels: none -> 12.6 us  [the longest x1 9.44 us: key_sums(): pl.pallas_call(key_kernel, in_specs=[vmem, vmem], out_specs=vmem, out_sha...]
    all_to_all x0 -> x1, waiting for transfers between devices: none -> 9.95 us  [spread(): return lax.all_to_all(blocks, AXES, 0, 0, tiled=True)]
    all_to_all x0 -> x1, starting transfers between devices: none -> 7.33 us  [spread(): return lax.all_to_all(blocks, AXES, 0, 0, tiled=True)]
  transfers between devices with their start and end apart: 2 -> 1, of which waited for: 2 -> 1; matrix products, arithmetic and copies ran while one was open for 0% -> 1% of each run, Pallas kernels for 0% -> 0%
where the time goes in v1:
time: 45.2 us; the launch traced here: 44.9 us
  blocking collectives  13.2 us (29%)
  Pallas kernels  12.6 us (28%)
  waiting for transfers between devices  9.95 us (22%)
  starting transfers between devices  7.33 us (16%)
  local copies, waits for them, and re-layouts  1.3 us (3%)
  other arithmetic  0.63 us (1%)
    all_to_all x1, blocking collectives, spread(): return lax.all_to_all(blocks, AXES, 0, 0, tiled=True)  13.2 us
    all_to_all x1, waiting for transfers between devices, spread(): return lax.all_to_all(blocks, AXES, 0, 0, tiled=True)  9.95 us
    pallas_call x1, Pallas kernels, key_sums(): pl.pallas_call(key_kernel, in_specs=[vmem, vmem], out_specs=vmem, out_sha...  9.44 us
    all_to_all x1, starting transfers between devices, spread(): return lax.all_to_all(blocks, AXES, 0, 0, tiled=True)  7.33 us
    pallas_call x1, Pallas kernels, category_sums(): pl.pallas_call(category_kernel, in_specs=[vmem, vmem, vmem, vmem], out_sp...  3.12 us
  transfers between devices with their start and end apart: 1, of which 1 were waited for; matrix products, arithmetic and copies ran while one was open for 1% of the time, Pallas kernels for 0%

profile of v1, /device:TPU:0, one launch (start us, length us, event | category | flops | bytes accessed | tf_op | source)
XLA Modules:
  0.0 44.9 jit_solution(14723409111822250651)
XLA Ops:
  0.0 0.0 copy-start
  0.0 9.4 %key_sums.1 = f32[256,256]{1,0:T(8,128)} custom-call(s32[256,128]{1,0:T(8,128)} %bitcast.7, bf16[256,128]{1,0:T(8,128)(2,1)} %bitcast.8), custom_call_target="tpu_custom_call" | custom-call | tf_op jit(solution)/shard_map/key_sums/pallas_call | solution.py:58
  9.4 7.3 %all-to-all-start = ((f32[32,8,256]{2,1,0:T(8,128)}), f32[32,8,256]{2,1,0:T(8,128)S(1)}, u32[]{:S(2)}, u32[]{:S(2)}) async-start(f32[32,8,256]{2,1,0:T(8,128)} %bitcast.5), calls=%async_computation | async-start | bytes 524288 | tf_op jit(solution)/shard_map/all_to_all | solution.py:109
  16.8 0.0 copy-done
  16.8 0.6 %constant_dynamic-slice_fusion.filt_ref = s32[8,256]{1,0:T(8,128)} fusion(s32[256,256]{1,0:T(8,128)S(1)} %copy-done, s32[]{:T(128)S(6)} %select_n.3), kind=kLoop, calls=%fused_computation | loop fusion | bytes 16388 | tf_op jit(solution)/shard_map/dynamic_slice | solution.py:115
  17.4 10.0 %all-to-all-done.terms_ref = f32[32,8,256]{2,1,0:T(8,128)S(1)} async-done(((f32[32,8,256]{2,1,0:T(8,128)}), f32[32,8,256]{2,1,0:T(8,128)S(1)}, u32[]{:S(2)}, u32[]{:S(2)}) %all-to-all-start) | async-done | bytes 262176 | tf_op jit(solution)/shard_map/all_to_all | solution.py:109
  27.4 0.0 copy-start.1
  27.4 0.7 %copy-done.1 = f32[32,8,256]{2,1,0:T(8,128)} copy-done((f32[32,8,256]{2,1,0:T(8,128)}, f32[32,8,256]{2,1,0:T(8,128)S(1)}, u32[]{:S(2)}) %copy-start.1) | copy-done | bytes 262168
  28.0 3.1 %category_sums.1 = f32[512,128]{1,0:T(8,128)} custom-call(f32[32,8,256]{2,1,0:T(8,128)} %copy-done.1, s32[8,256]{1,0:T(8,128)} %constant_dynamic-slice_fusion.filt_ref, s32[16,128]{1,0:T(8,128)} %bitcast.9, bf16[2048,128]{1,0:T(8,128)(2,1)} %attrs_ref.1), custom_call_target="tpu_custom_call" | custom-call | tf_op jit(solution)/shard_map/category_sums/pallas_call | solution.py:95
  31.2 13.2 %all_to_all.10 = f32[32,16,128]{2,1,0:T(8,128)S(1)} all-to-all(f32[32,16,128]{2,1,0:T(8,128)} %bitcast.6), channel_id=1, replica_groups=mesh['fact'=8,'dim'=4] {'fact','dim'}, dimensions={0} | all-to-all | bytes 524288 | tf_op jit(solution)/shard_map/all_to_all | solution.py:109
  44.3 0.6 %reduce_sum.9 = f32[16,128]{1,0:T(8,128)} reduce(f32[32,16,128]{2,1,0:T(8,128)S(1)} %all_to_all.10, f32[]{:T(128)} %constant.18.clone.1), dimensions={0}, to_apply=%region_0.0 | reduce | flops 63488 | bytes 270340 | tf_op jit(solution)/shard_map/reduce_sum | solution.py:117
Async XLA Ops:
  0.0 16.8 %copy-start = (s32[256,256]{1,0:T(8,128)S(1)}, s32[256,256]{1,0:T(8,128)}, u32[]{:S(2)}) copy-start(s32[256,256]{1,0:T(8,128)} %param.7) | copy-start | bytes 786436
  9.4 17.9 %all-to-all-start = ((f32[32,8,256]{2,1,0:T(8,128)}), f32[32,8,256]{2,1,0:T(8,128)S(1)}, u32[]{:S(2)}, u32[]{:S(2)}) async-start(f32[32,8,256]{2,1,0:T(8,128)} %bitcast.5), calls=%async_computation | async-start | bytes 524288 | tf_op jit(solution)/shard_map/all_to_all | solution.py:109
  27.4 0.7 %copy-start.1 = (f32[32,8,256]{2,1,0:T(8,128)}, f32[32,8,256]{2,1,0:T(8,128)S(1)}, u32[]{:S(2)}) copy-start(f32[32,8,256]{2,1,0:T(8,128)S(1)} %all-to-all-done.terms_ref) | copy-start | bytes 786436

commit v2 on v1

--- a/solution.py
+++ b/solution.py
@@ -9,7 +9,7 @@
 AXES = ("fact", "dim")
 LANES = 128
 SUB = 16
-CHUNK = 16
+CHUNK = 128
 
 
 def hot(values, size):
@@ -59,46 +59,50 @@
         key_kernel,
         in_specs=[vmem, vmem],
         out_specs=vmem,
-        out_shape=jax.ShapeDtypeStruct((key_hi, key_lo), jnp.float32),
+        out_shape=pltpu.VMEM((key_hi, key_lo), jnp.float32),
         name="key_sums",
     )(fact_keys.reshape(-1, LANES), revenue.reshape(-1, LANES))
 
 
 def category_kernel(terms_ref, filt_ref, cats_ref, attrs_ref, out_ref):
-    half = out_ref.shape[0] // 2
+    size, width = out_ref.shape
+    half = size // 2
     cats = cats_ref[...]
     sums = jnp.where(filt_ref[...] == 1, jnp.sum(terms_ref[...], axis=0), 0.0)
-    coarse = sums.astype(jnp.bfloat16).astype(jnp.float32)
-    fine = sums - coarse
+    parts = sums.shape[1] // LANES
+    one = jnp.ones((), jnp.bfloat16)
     zero = jnp.zeros((), jnp.bfloat16)
-    parts = sums.shape[1] // LANES
-    for part in range(2):
-        lhs, rhs = [], []
-        for j in range(cats.shape[0]):
-            r, c = j // parts, (j % parts) * LANES
-            mask = hot(cats[j : j + 1] - part * half, half)
-            attrs = attrs_ref[j * LANES : (j + 1) * LANES, :]
-            for piece in (coarse, fine):
-                row = jnp.broadcast_to(piece[r : r + 1, c : c + LANES], (SUB, LANES))
-                row = row.astype(jnp.bfloat16)[None]
-                lhs.append(jnp.where(mask, row, zero).reshape(half, LANES))
-                rhs.append(attrs)
-        out_ref[part * half : (part + 1) * half, :] = jnp.dot(
-            jnp.concatenate(lhs, axis=1),
-            jnp.concatenate(rhs, axis=0),
-            preferred_element_type=jnp.float32,
+    lhs, rhs = [], []
+    for j in range(cats.shape[0]):
+        r, c = j // parts, (j % parts) * LANES
+        masks = [hot(cats[j : j + 1] - part * half, half) for part in range(2)]
+        lhs.append(
+            jnp.concatenate([jnp.where(m, one, zero).reshape(half, LANES) for m in masks], axis=0)
         )
+        column = jnp.broadcast_to(sums[r : r + 1, c : c + LANES], (LANES, LANES)).T
+        attrs = attrs_ref[j * LANES : (j + 1) * LANES, :].astype(jnp.float32)
+        weighted = column * attrs
+        coarse = weighted.astype(jnp.bfloat16)
+        fine = (weighted - coarse.astype(jnp.float32)).astype(jnp.bfloat16)
+        rhs.append(jnp.concatenate([coarse, fine], axis=1))
+    both = jnp.dot(
+        jnp.concatenate(lhs, axis=1),
+        jnp.concatenate(rhs, axis=0),
+        preferred_element_type=jnp.float32,
+    )
+    out_ref[...] = both[:, :width] + both[:, width:]
 
 
 def category_sums(terms, filt, categories, attributes):
+    args = (terms, filt, categories.reshape(-1, LANES), attributes)
     vmem = pl.BlockSpec(memory_space=pltpu.VMEM)
     return pl.pallas_call(
         category_kernel,
         in_specs=[vmem, vmem, vmem, vmem],
         out_specs=vmem,
-        out_shape=jax.ShapeDtypeStruct((CATS, attributes.shape[1]), jnp.float32),
+        out_shape=pltpu.VMEM((CATS, attributes.shape[1]), jnp.float32),
         name="category_sums",
-    )(terms, filt, categories.reshape(-1, LANES), attributes)
+    )(*(pltpu.with_memory_space_constraint(x, pltpu.VMEM) for x in args))
 
 
 def solution(mesh):

time: 45.2 us -> 38.8 us (0.86)
  Pallas kernels: 12.6 us -> 7.29 us
  local copies, waits for them, and re-layouts: 1.3 us -> 0.02 us
  waiting for transfers between devices: 9.95 us -> 10.5 us
    pallas_call x1, Pallas kernels: 9.44 us -> 6.43 us  [key_sums(): pl.pallas_call(key_kernel, in_specs=[vmem, vmem], out_specs=vmem, out_sha...]
    pallas_call x1, Pallas kernels: 3.12 us -> 0.86 us  [category_sums(): pl.pallas_call(category_kernel, in_specs=[vmem, vmem, vmem, vmem], out_sp...]
    unnamed x4 -> x6, local copies, waits for them, and re-layouts: 0.69 us -> 0.01 us
    dynamic_slice x1, local copies, waits for them, and re-layouts: 0.61 us -> 0.01 us  [per_device(): lax.dynamic_slice_in_dim(filter_bits, lax.axis_index(AXES) * rows, rows, 0)]
    all_to_all x1, waiting for transfers between devices: 9.95 us -> 10.5 us  [spread(): return lax.all_to_all(blocks, AXES, 0, 0, tiled=True)]
  transfers between devices with their start and end apart: 1 -> 1, of which waited for: 1 -> 1; matrix products, arithmetic and copies ran while one was open for 1% -> 0% of each run, Pallas kernels for 0% -> 0%
where the time goes in v2:
time: 38.8 us; the launch traced here: 38.6 us
  blocking collectives  12.8 us (33%)
  waiting for transfers between devices  10.5 us (27%)
  starting transfers between devices  7.32 us (19%)
  Pallas kernels  7.29 us (19%)
  other arithmetic  0.63 us (2%)
    all_to_all x1, blocking collectives, spread(): return lax.all_to_all(blocks, AXES, 0, 0, tiled=True)  12.8 us
    all_to_all x1, waiting for transfers between devices, spread(): return lax.all_to_all(blocks, AXES, 0, 0, tiled=True)  10.5 us
    all_to_all x1, starting transfers between devices, spread(): return lax.all_to_all(blocks, AXES, 0, 0, tiled=True)  7.32 us
    pallas_call x1, Pallas kernels, key_sums(): pl.pallas_call(key_kernel, in_specs=[vmem, vmem], out_specs=vmem, out_sha...  6.43 us
    pallas_call x1, Pallas kernels, category_sums(): pl.pallas_call(category_kernel, in_specs=[vmem, vmem, vmem, vmem], out_sp...  0.86 us
  transfers between devices with their start and end apart: 1, of which 1 were waited for; matrix products, arithmetic and copies ran while one was open for 0% of the time, Pallas kernels for 0%

profile of v2, /device:TPU:0, one launch (start us, length us, event | category | flops | bytes accessed | tf_op | source)
XLA Modules:
  0.0 38.6 jit_solution(5471326458258781525)
XLA Ops:
  0.0 0.0 copy-start
  0.0 0.0 copy-start.1
  0.0 6.4 %key_sums.1 = f32[256,256]{1,0:T(8,128)} custom-call(s32[256,128]{1,0:T(8,128)} %bitcast.7, bf16[256,128]{1,0:T(8,128)(2,1)} %bitcast.8), custom_call_target="tpu_custom_call" | custom-call | tf_op jit(solution)/shard_map/key_sums/pallas_call | solution.py:58
  6.4 7.3 %all-to-all-start = ((f32[32,8,256]{2,1,0:T(8,128)}), f32[32,8,256]{2,1,0:T(8,128)S(1)}, u32[]{:S(2)}, u32[]{:S(2)}) async-start(f32[32,8,256]{2,1,0:T(8,128)} %bitcast.2), calls=%async_computation | async-start | bytes 524288 | tf_op jit(solution)/shard_map/all_to_all | solution.py:113
  13.8 0.0 copy-done
  13.8 0.0 copy-start.2
  13.8 10.5 %all-to-all-done.terms_ref = f32[32,8,256]{2,1,0:T(8,128)S(1)} async-done(((f32[32,8,256]{2,1,0:T(8,128)}), f32[32,8,256]{2,1,0:T(8,128)S(1)}, u32[]{:S(2)}, u32[]{:S(2)}) %all-to-all-start) | async-done | bytes 262176 | tf_op jit(solution)/shard_map/all_to_all | solution.py:113
  24.3 0.0 copy-done.1
  24.3 0.0 copy-done.2
  24.3 0.9 %category_sums.1 = f32[512,128]{1,0:T(8,128)S(1)} custom-call(f32[32,8,256]{2,1,0:T(8,128)S(1)} %all-to-all-done.terms_ref, s32[8,256]{1,0:T(8,128)S(1)} %constant_dynamic-slice_fusion.filt_ref, s32[16,128]{1,0:T(8,128)S(1)} %bitcast.6, bf16[2048,128]{1,0:T(8,128)(2,1)S(1)} %copy-done.1), custom_call_target="tpu_custom_call" | custom-call | tf_op jit(solution)/shard_map/category_sums/pallas_call | solution.py:99
  25.2 12.8 %all_to_all.10 = f32[32,16,128]{2,1,0:T(8,128)S(1)} all-to-all(f32[32,16,128]{2,1,0:T(8,128)S(1)} %bitcast.5), channel_id=1, replica_groups=mesh['fact'=8,'dim'=4] {'fact','dim'}, dimensions={0} | all-to-all | bytes 524288 | tf_op jit(solution)/shard_map/all_to_all | solution.py:113
  38.0 0.6 %reduce_sum.9 = f32[16,128]{1,0:T(8,128)} reduce(f32[32,16,128]{2,1,0:T(8,128)S(1)} %all_to_all.10, f32[]{:T(128)} %constant.18.clone.1), dimensions={0}, to_apply=%region_0.0 | reduce | flops 63488 | bytes 270340 | tf_op jit(solution)/shard_map/reduce_sum | solution.py:121
  (1 shorter events, 0.0 us)
Async XLA Ops:
  0.0 13.8 %copy-start = (s32[256,256]{1,0:T(8,128)S(1)}, s32[256,256]{1,0:T(8,128)}, u32[]{:S(2)}) copy-start(s32[256,256]{1,0:T(8,128)} %param.7) | copy-start | bytes 786436
  0.0 24.3 %copy-start.1 = (bf16[2048,128]{1,0:T(8,128)(2,1)S(1)}, bf16[2048,128]{1,0:T(8,128)(2,1)}, u32[]{:S(2)}) copy-start(bf16[2048,128]{1,0:T(8,128)(2,1)} %attrs_ref.1) | copy-start | bytes 1572868
  6.4 17.9 %all-to-all-start = ((f32[32,8,256]{2,1,0:T(8,128)}), f32[32,8,256]{2,1,0:T(8,128)S(1)}, u32[]{:S(2)}, u32[]{:S(2)}) async-start(f32[32,8,256]{2,1,0:T(8,128)} %bitcast.2), calls=%async_computation | async-start | bytes 524288 | tf_op jit(solution)/shard_map/all_to_all | solution.py:113
  13.8 10.6 %copy-start.2 = (s32[2048]{0:T(1024)S(1)}, s32[2048]{0:T(1024)}, u32[]{:S(2)}) copy-start(s32[2048]{0:T(1024)} %param.8) | copy-start | bytes 24580
